TPU v7x, 32 devices: a whole 2x2x4 slice. The times are simulated.
32 devices in a mesh: head: 8 (over z, x), client: 4 (over y, core).
Axes of the slice: x: 2, y: 2, z: 4, core: 2. Of those that a mesh axis runs over, the one named last changes fastest.
Arguments:
- client_ids: int32 [32], replicated, may hold values from 0 to 127, as said below
- client_table: bfloat16 [128, 256], replicated, may hold values from -6 to 6
- in_weight: bfloat16 [256, 4096], P(None, 'client'), may hold values from -0.375 to 0.375
- in_bias: float32 [4096], P('client'), may hold values from -3 to 3
- head_weight: bfloat16 [4096, 131072], P('client', 'head'), may hold values from -0.09375 to 0.09375
- tokens: int32 [32, 256], P(('head', 'client')), may hold values from 0 to 255
- labels: int32 [32, 256], P(('head', 'client')), may hold values from 0 to 255
- byte_table: bfloat16 [256, 4096], P(None, 'client'), may hold values from -5.5 to 6.7
- out_table: bfloat16 [256, 4096], P(None, 'client'), may hold values from -5.625 to 5.625
Outputs:
- head_grad: bfloat16 [4096, 131072], P('client', 'head')
- in_grad: float32 [256, 4096], P(None, 'client')
- losses: float32 [32], P(('head', 'client'))
Inputs may be any that keep to these rules, and one draw needn't show every extreme that they name: `client_ids`: distinct population indices.
All inputs are finite; a program needn't handle non-finite values.
Results may differ from a plain program's by a relative error of at most 0.0085.
Values may be sent and summed in bfloat16 or wider, within the bound.
A program may use at most 128 MiB of HBM per device.

v0:
```python
import jax
import jax.numpy as jnp
from jax import lax
from jax.sharding import PartitionSpec as P

EPSILON = 1e-06
learn_rate = 0.1


def client_loss(factor_a, factor_b, inputs, label_row, out_table):
    depth = factor_a.shape[0]
    rank_size = factor_a.shape[1]
    normed_in = inputs * lax.rsqrt(jnp.mean(inputs * inputs, -1, keepdims=True) + EPSILON)
    low_rank = jnp.dot(normed_in, factor_a, precision=lax.Precision.HIGHEST)
    adapted = inputs + jnp.dot(low_rank, factor_b, precision=lax.Precision.HIGHEST) / jnp.sqrt(
        jnp.float32(depth * rank_size)
    )
    normed = (adapted * lax.rsqrt(jnp.mean(adapted * adapted, -1, keepdims=True) + EPSILON)).astype(
        jnp.bfloat16
    )
    logits = lax.dot_general(
        normed, out_table, (((1,), (1,)), ((), ())), preferred_element_type=jnp.float32
    )
    logits = logits * (4.0 / jnp.sqrt(jnp.float32(depth)))
    log_total = jax.nn.logsumexp(logits, -1)
    vocab_ids = lax.broadcasted_iota(jnp.int32, logits.shape, 1)
    picked = jnp.sum(jnp.where(vocab_ids == label_row[:, None], logits, 0.0), -1)
    return jnp.sum(log_total - picked)


def train_client(factor_row, token_row, label_row, byte_table, out_table):
    depth = byte_table.shape[1]
    split_at = factor_row.shape[0] // 2
    rank_size = split_at // depth
    start_a = factor_row[:split_at].reshape(depth, rank_size).astype(jnp.float32)
    start_b = factor_row[split_at:].reshape(rank_size, depth).astype(jnp.float32)
    onehot = (
        token_row[:, None]
        == lax.broadcasted_iota(jnp.int32, (token_row.shape[0], byte_table.shape[0]), 1)
    ).astype(jnp.bfloat16)
    inputs = jnp.dot(onehot, byte_table, preferred_element_type=jnp.float32)
    loss_grad = jax.value_and_grad(client_loss, argnums=(0, 1))
    first_loss, (grad_a, grad_b) = loss_grad(start_a, start_b, inputs, label_row, out_table)
    middle_a = start_a - learn_rate * grad_a
    middle_b = start_b - learn_rate * grad_b
    second_loss, (grad_a, grad_b) = loss_grad(middle_a, middle_b, inputs, label_row, out_table)
    final_a = middle_a - learn_rate * grad_a
    final_b = middle_b - learn_rate * grad_b
    deltas = jnp.concatenate(
        [(final_a - start_a).reshape(-1), (final_b - start_b).reshape(-1)]
    ).astype(jnp.bfloat16)
    return (deltas, first_loss / token_row.shape[0])


def local(
    client_ids, client_table, in_weight, in_bias, head_weight, tokens, labels, byte_table, out_table
):
    head_count = lax.axis_size("head")
    group_count = lax.axis_size("client")
    per_device = tokens.shape[0]
    byte_full, out_full = (
        lax.all_gather(byte_table, "client", axis=1, tiled=True),
        lax.all_gather(out_table, "client", axis=1, tiled=True),
    )
    ordered = client_ids.reshape(head_count, group_count, per_device).transpose(1, 0, 2).reshape(-1)
    chosen = client_table[ordered]
    preact = jnp.dot(chosen, in_weight, preferred_element_type=jnp.float32) + in_bias
    hidden = jnp.maximum(preact, 0.0).astype(jnp.bfloat16)
    hidden_rows = hidden
    summed = lax.psum_scatter(
        jnp.dot(hidden_rows, head_weight, preferred_element_type=jnp.float32),
        "client",
        scatter_dimension=0,
        tiled=True,
    )
    owned = lax.all_to_all(
        summed.astype(jnp.bfloat16), "head", split_axis=0, concat_axis=1, tiled=True
    )

    def run_client(record):
        return train_client(record[0], record[1], record[2], byte_full, out_full)

    deltas, losses = lax.map(run_client, (owned, tokens, labels))
    returned = lax.all_to_all(deltas, "head", split_axis=1, concat_axis=0, tiled=True)
    received = lax.all_gather(returned, "client", axis=0, tiled=True)
    hidden_rows = hidden
    grad_sum = lax.dot_general(
        hidden_rows, received, (((0,), (0,)), ((), ())), preferred_element_type=jnp.float32
    )
    partial_value = lax.dot_general(
        received, head_weight, (((1,), (1,)), ((), ())), preferred_element_type=jnp.float32
    )
    hidden_back = partial_value
    grad_sum, hidden_back = (grad_sum, hidden_back)
    hidden_back = lax.psum(hidden_back, "head")
    masked = jnp.where(preact > 0, hidden_back, 0.0)
    in_grad = lax.dot_general(
        chosen.astype(jnp.float32),
        masked,
        (((0,), (0,)), ((), ())),
        precision=lax.Precision.HIGHEST,
    )
    return (grad_sum.astype(jnp.bfloat16), in_grad, losses)


def solution(mesh):
    placed = (
        P(),
        P(),
        P(None, "client"),
        P("client"),
        P("client", "head"),
        P(("head", "client"), None),
        P(("head", "client"), None),
        P(None, "client"),
        P(None, "client"),
    )
    return jax.shard_map(
        local,
        mesh=mesh,
        in_specs=placed,
        out_specs=(P("client", "head"), P(None, "client"), P(("head", "client"))),
        check_vma=False,
    )
```

profile of v0, /device:TPU:0, one launch (start us, length us, event | category | flops | bytes accessed | tf_op | source)
XLA Modules:
  0.0 274.1 jit_solution(7337150185194927193)
XLA Ops:
  8.2 1.5 gather_fusion
  10.5 14.9 %fusion.59 = f32[32,16384]{1,0:T(8,128)} fusion(bf16[1024,16384]{1,0:T(8,128)(2,1)} %param.13, f32[32,1024]{1,0:T(8,128)S(1)} %convolution_add_fusion), kind=kOutput, calls=%fused_computation.91 | convolution fusion | flops 1073807360 | bytes 35782656 | tf_op jit(solution)/shard_map/dot_general | solution.py:71
  26.9 32.6 %reduce-scatter.2.cloned.1.call-done = f32[8,16384]{1,0:T(8,128)} async-done(((f32[32,16384]{1,0:T(8,128)}), f32[8,16384]{1,0:T(8,128)}) %reduce-scatter.2.cloned.1.call-update) | async-done | bytes 524304 | tf_op jit(solution)/shard_map/reduce_scatter | solution.py:70
  59.5 1.1 convert_bitcast_fusion
  61.9 0.9 reshape.181
  62.8 5.5 %all-to-all-start = ((bf16[8,2,8192]{2,1,0:T(2,128)(2,1)}), bf16[8,2,8192]{2,1,0:T(2,128)(2,1)S(1)}, u32[]{:S(2)}, u32[]{:S(2)}) async-start(bf16[8,2,8192]{2,1,0:T(2,128)(2,1)} %reshape.181), calls=%async_computation.1 | async-start | bytes 524288 | tf_op jit(solution)/shard_map/all_to_all | solution.py:76
  68.3 15.3 %all-gather.5.cloned.1.call-done = bf16[256,4096]{1,0:T(8,128)(2,1)} async-done(((bf16[256,1024]{1,0:T(8,128)(2,1)}), bf16[256,4096]{1,0:T(8,128)(2,1)}) %all-gather.5.cloned.1.call-update) | async-done | bytes 2097168 | tf_op jit(solution)/shard_map/all_gather | solution.py:62
  83.7 4.4 %multiply_reduce_fusion.2 = (f32[256]{0:T(256)S(1)}, f32[256,4096]{1,0:T(8,128)}) fusion(bf16[256,4096]{1,0:T(8,128)(2,1)} %all-gather.5.cloned.1.call-done, s32[256]{0:T(256)S(1)} %bitcast.43), kind=kOutput, calls=%fused_computation.34 | convolution fusion | flops 539033344 | bytes 6293504 | tf_op jit(solution)/shard_map/while/body/eval_jaxpr/dot_general | solution.py:41
  88.8 1.2 slice_reduce_fusion
  91.2 5.0 %fusion.18 = f32[256,16]{0,1:T(8,128)S(1)} fusion(bf16[4096,16]{1,0:T(8,128)(2,1)S(1)} %reshape.168, f32[256,4096]{1,0:T(8,128)} %get-tuple-element.34, f32[256]{0:T(256)S(1)} %add_rsqrt_fusion), kind=kOutput, calls=%fused_computation.39 | convolution fusion | flops 202375168 | bytes 4342784 | tf_op jit(solution)/shard_map/while/body/eval_jaxpr/jvp()/dot_general | solution.py:14
  96.3 4.3 %multiply_reduce_fusion.1 = (f32[256]{0:T(256)S(1)}, f32[256,4096]{1,0:T(8,128)}) fusion(f32[256,4096]{1,0:T(8,128)S(1)} %copy-done.2, f32[256,16]{0,1:T(8,128)S(1)} %fusion.18, bf16[16,4096]{1,0:T(8,128)(2,1)S(1)} %reshape.169), kind=kOutput, calls=%fused_computation.33 | convolution fusion | flops 205520640 | bytes 8537088 | tf_op jit(solution)/shard_map/while/body/eval_jaxpr/jvp()/dot_general | solution.py:15
  100.6 7.2 %all-gather.7.cloned.1.call-done = bf16[256,4096]{1,0:T(8,128)(2,1)} async-done(((bf16[256,1024]{1,0:T(8,128)(2,1)}), bf16[256,4096]{1,0:T(8,128)(2,1)}) %all-gather.7.cloned.1.call-update) | async-done | bytes 2097168 | tf_op jit(solution)/shard_map/all_gather | solution.py:63
  107.8 3.9 %fusion.78 = (f32[256]{0:T(256)S(1)}, f32[256,256]{0,1:T(8,128)S(1)}) fusion(bf16[256,4096]{1,0:T(8,128)(2,1)} %all-gather.7.cloned.1.call-done, f32[256,4096]{1,0:T(8,128)} %get-tuple-element.36, f32[256]{0:T(256)S(1)} %fusion.60), kind=kOutput, calls=%fused_computation.118 | convolution fusion | flops 539098880 | bytes 6555648 | tf_op jit(solution)/shard_map/while/body/eval_jaxpr/jvp()/dot_general | solution.py:21
  112.5 0.9 fusion.10
  113.5 2.8 %fusion.76 = f32[256,16]{0,1:T(8,128)S(1)} fusion(bf16[16,4096]{1,0:T(8,128)(2,1)S(1)} %reshape.169, bf16[256,4096]{1,0:T(8,128)(2,1)S(1)} %get-tuple-element.40, f32[256,4096]{1,0:T(8,128)S(1)} %copy-done.4, f32[256]{0:T(256)S(1)} %multiply_multiply_fusion.1, f32[256]{0:T(256)S(1)} %fusion.60), kind=kOutput, calls=%fused_computation.117 | convolution fusion | flops 207618048 | bytes 6440960 | tf_op jit(solution)/shard_map/while/body/eval_jaxpr/transpose(jvp())/dot_general | solution.py:15
  116.3 3.1 %fusion.6 = f32[16,4096]{1,0:T(8,128)S(1)} fusion(f32[256,16]{0,1:T(8,128)S(1)} %fusion.18, bf16[16,4096]{1,0:T(8,128)(2,1)S(1)} %reshape.169, bf16[256,4096]{1,0:T(8,128)(2,1)S(1)} %get-tuple-element.40, f32[256,4096]{1,0:T(8,128)S(1)} %copy-done.4, f32[256]{0:T(256)S(1)} %multiply_multiply_fusion.1, f32[256]{0:T(256)S(1)} %fusion.60), kind=kOutput, calls=%fused_computation.21 | convolution fusion | flops 207814656 | bytes 6703104 | tf_op jit(solution)/shard_map/while/body/eval_jaxpr/transpose(jvp())/dot_general | solution.py:15
  119.4 2.5 fusion.7
  121.9 3.4 %fusion.15 = f32[256,16]{0,1:T(8,128)S(1)} fusion(f32[4096,16]{0,1:T(8,128)S(1)} %fusion.7, f32[256,4096]{1,0:T(8,128)S(1)} %copy-done.3, f32[256]{0:T(256)S(1)} %add_rsqrt_fusion), kind=kOutput, calls=%fused_computation.36 | convolution fusion | flops 202375168 | bytes 4473856 | tf_op jit(solution)/shard_map/while/body/eval_jaxpr/jvp()/dot_general | solution.py:14
  125.4 4.1 %multiply_reduce_fusion = (f32[256]{0:T(256)S(1)}, f32[256,4096]{1,0:T(8,128)S(1)}) fusion(f32[256,4096]{1,0:T(8,128)S(1)} %copy-done.3, f32[256,16]{0,1:T(8,128)S(1)} %fusion.15, f32[16,4096]{1,0:T(8,128)S(1)} %fusion.6), kind=kOutput, calls=%fused_computation.31 | convolution fusion | flops 205520640 | bytes 8668160 | tf_op jit(solution)/shard_map/while/body/eval_jaxpr/jvp()/dot_general | solution.py:15
  130.4 0.9 fusion.11
  131.4 4.2 %fusion.73 = f32[256,16]{0,1:T(8,128)S(1)} fusion(f32[16,4096]{1,0:T(8,128)S(1)} %fusion.6, bf16[256,4096]{1,0:T(8,128)(2,1)S(1)} %get-tuple-element.46, f32[256,4096]{1,0:T(8,128)S(1)} %get-tuple-element.42, f32[256]{0:T(256)S(1)} %multiply_multiply_fusion, f32[256]{0:T(256)S(1)} %fusion.61), kind=kOutput, calls=%fused_computation.116 | convolution fusion | flops 207618048 | bytes 6572032 | tf_op jit(solution)/shard_map/while/body/eval_jaxpr/transpose(jvp())/dot_general | solution.py:15
  135.6 2.9 %fusion.9 = bf16[16,4096]{1,0:T(8,128)(2,1)S(1)} fusion(f32[16,4096]{1,0:T(8,128)S(1)} %fusion.6, f32[256,16]{0,1:T(8,128)S(1)} %fusion.15, bf16[16,4096]{1,0:T(8,128)(2,1)S(1)} %reshape.169, bf16[256,4096]{1,0:T(8,128)(2,1)S(1)} %get-tuple-element.46, f32[256,4096]{1,0:T(8,128)S(1)} %get-tuple-element.42, f32[256]{0:T(256)S(1)} %multiply_multiply_fusion, ...), kind=kOutput, calls=%fused_computation.25 | convolution fusion | flops 207945728 | bytes 6834176 | tf_op jit(solution)/shard_map/while/body/eval_jaxpr/transpose(jvp())/dot_general | solution.py:15
  138.5 2.5 fusion.8
  141.5 1.2 concatenate.17
  143.4 2.2 reduce.5
  145.8 14.9 %all_to_all.26 = bf16[8,2,8192]{2,1,0:T(2,128)(2,1)S(1)} all-to-all(bf16[8,2,8192]{2,1,0:T(2,128)(2,1)S(1)} %reshape.183), channel_id=1, replica_groups=mesh['head'=8,'client'=4] {'head'}, dimensions={0} | all-to-all | bytes 524288 | tf_op jit(solution)/shard_map/all_to_all | solution.py:84
  161.0 1.0 copy.27
  162.6 14.3 %all-gather.9.cloned.1.call-done = bf16[1,32,16384]{2,1,0:T(8,128)(2,1)} async-done(((bf16[1,8,16384]{2,1,0:T(8,128)(2,1)}), bf16[1,32,16384]{2,1,0:T(8,128)(2,1)}) %all-gather.9.cloned.1.call-update) | async-done | bytes 1048592 | tf_op jit(solution)/shard_map/all_gather | solution.py:85
  177.0 16.1 %fusion.30 = f32[32,1024]{1,0:T(8,128)} fusion(bf16[1024,16384]{1,0:T(8,128)(2,1)} %param.13, bf16[1,32,16384]{2,1,0:T(8,128)(2,1)} %all-gather.9.cloned.1.call-done), kind=kOutput, calls=%fused_computation.52 | convolution fusion | flops 1073741824 | bytes 34734080 | tf_op jit(solution)/shard_map/dot_general | solution.py:90
  193.1 14.9 %convolution_convert_fusion = bf16[1024,16384]{1,0:T(8,128)(2,1)} fusion(bf16[1,32,16384]{2,1,0:T(8,128)(2,1)S(1)} %copy-done.6, f32[32,1024]{1,0:T(8,128)S(1)} %convolution_add_fusion), kind=kOutput, calls=%fused_computation.1 | convolution fusion | flops 1090584576 | bytes 34734080 | tf_op jit(solution)/shard_map/dot_general | solution.py:87
  207.9 55.7 %all-reduce.2.cloned.1.call-done = f32[32,1024]{1,0:T(8,128)} async-done(((f32[32,1024]{1,0:T(8,128)}), f32[32,1024]{1,0:T(8,128)}) %all-reduce.2.cloned.1.call-update) | async-done | bytes 131088 | tf_op jit(solution)/shard_map/psum | solution.py:95
  263.7 2.5 fusion.42
  (59 shorter events, 10.3 us)
Async XLA Ops:
  7.2 2.5 copy-start
  7.2 52.3 %reduce-scatter.2.cloned.1.call-start = ((), (), s32[]{:S(2)}) async-start(), calls=%async_computation.3 | async-start | bytes 2621440 | tf_op jit(solution)/shard_map/reduce_scatter | solution.py:70
  25.4 58.2 %copy-start.7 = (s32[1,256]{1,0:T(1,128)S(1)}, s32[1,256]{1,0:T(1,128)}, u32[]{:S(2)}) copy-start(s32[1,256]{1,0:T(1,128)} %param.14) | copy-start | bytes 3076
  25.4 58.2 %all-gather.5.cloned.1.call-start = ((), (), s32[]{:S(2)}) async-start(), calls=%async_computation.4 | async-start | bytes 2621440 | tf_op jit(solution)/shard_map/all_gather | solution.py:62
  26.2 81.6 %all-gather.7.cloned.1.call-start = ((), (), s32[]{:S(2)}) async-start(), calls=%async_computation.5 | async-start | bytes 2621440 | tf_op jit(solution)/shard_map/all_gather | solution.py:63
  62.8 25.2 %all-to-all-start = ((bf16[8,2,8192]{2,1,0:T(2,128)(2,1)}), bf16[8,2,8192]{2,1,0:T(2,128)(2,1)S(1)}, u32[]{:S(2)}, u32[]{:S(2)}) async-start(bf16[8,2,8192]{2,1,0:T(2,128)(2,1)} %reshape.181), calls=%async_computation.1 | async-start | bytes 524288 | tf_op jit(solution)/shard_map/all_to_all | solution.py:76
  68.3 108.7 %all-gather.9.cloned.1.call-start = ((), (), s32[]{:S(2)}) async-start(), calls=%async_computation.7 | async-start | bytes 1310720 | tf_op jit(solution)/shard_map/all_gather | solution.py:85
  91.2 5.1 %copy-start.2 = (f32[256,4096]{1,0:T(8,128)S(1)}, f32[256,4096]{1,0:T(8,128)}, u32[]{:S(2)}) copy-start(f32[256,4096]{1,0:T(8,128)} %get-tuple-element.34) | copy-start | bytes 12582916
  100.6 11.1 %copy-start.8 = (s32[1,256]{1,0:T(1,128)S(1)}, s32[1,256]{1,0:T(1,128)}, u32[]{:S(2)}) copy-start(s32[1,256]{1,0:T(1,128)} %param.15) | copy-start | bytes 3076
  107.8 4.6 %copy-start.4 = (f32[256,4096]{1,0:T(8,128)S(1)}, f32[256,4096]{1,0:T(8,128)}, u32[]{:S(2)}) copy-start(f32[256,4096]{1,0:T(8,128)} %get-tuple-element.36) | copy-start | bytes 12582916
  107.8 4.7 %copy-start.5 = (bf16[256,4096]{1,0:T(8,128)(2,1)S(1)}, bf16[256,4096]{1,0:T(8,128)(2,1)}, u32[]{:S(2)}) copy-start(bf16[256,4096]{1,0:T(8,128)(2,1)} %all-gather.7.cloned.1.call-done) | copy-start | bytes 6291460
  116.3 3.1 %copy-start.3 = (f32[256,4096]{1,0:T(8,128)S(1)}, f32[256,4096]{1,0:T(8,128)}, u32[]{:S(2)}) copy-start(f32[256,4096]{1,0:T(8,128)} %get-tuple-element.34) | copy-start | bytes 12582916
  162.0 101.7 %all-reduce.2.cloned.1.call-start = ((), (), s32[]{:S(2)}) async-start(), calls=%async_computation.6 | async-start | bytes 262144 | tf_op jit(solution)/shard_map/psum | solution.py:95
  177.0 16.1 %copy-start.6 = (bf16[1,32,16384]{2,1,0:T(8,128)(2,1)S(1)}, bf16[1,32,16384]{2,1,0:T(8,128)(2,1)}, u32[]{:S(2)}) copy-start(bf16[1,32,16384]{2,1,0:T(8,128)(2,1)} %all-gather.9.cloned.1.call-done) | copy-start | bytes 3145732
  193.1 73.1 %copy-start.1 = (bf16[256,1024]{1,0:T(8,128)(2,1)S(1)}, bf16[256,1024]{1,0:T(8,128)(2,1)}, u32[]{:S(2)}) copy-start(bf16[256,1024]{1,0:T(8,128)(2,1)} %param.11) | copy-start | bytes 1572868
Sparse Core Ops, SparseCore 0:
  25.6 33.9 reduce-scatter.1
  61.1 22.5 all-gather.4
  85.2 22.5 all-gather.6
  162.1 14.7 all-gather.8
  193.2 70.4 all-reduce.1
where the time goes:
time: 278 us; the launch traced here: 274 us
  waiting for transfers between devices  127 us (46%)
  matrix products  95 us (34%)
  between operations  15.9 us (6%)
  blocking collectives  14.9 us (5%)
  local copies, waits for them, and re-layouts  10.8 us (4%)
  starting transfers between devices  5.69 us (2%)
  other arithmetic  5.08 us (2%)
    psum x1, waiting for transfers between devices, local(): hidden_back = lax.psum(hidden_back, 'head')  55.7 us
    reduce_scatter x1, waiting for transfers between devices, local(): lax.psum_scatter(jnp.dot(hidden_rows, head_weight, preferred_element_type...  32.6 us
    dot_general x6, matrix products, client_loss(): jnp.dot(low_rank, factor_b, precision=lax.Precision.HIGHEST)  21.5 us
    dot_general x1, matrix products, local(): lax.dot_general(received, head_weight, (((1,), (1,)), ((), ())), preferre...  16.1 us
    all_gather x1, waiting for transfers between devices, local(): lax.all_gather(byte_table, 'client', axis=1, tiled=True)  15.3 us
    all_to_all x1, blocking collectives, local(): lax.all_to_all(deltas, 'head', split_axis=1, concat_axis=0, tiled=True)  14.9 us
    dot_general x1, matrix products, local(): lax.dot_general(hidden_rows, received, (((0,), (0,)), ((), ())), preferre...  14.9 us
    dot_general x1, matrix products, local(): jnp.dot(hidden_rows, head_weight, preferred_element_type=jnp.float32)  14.9 us
  transfers between devices with their start and end apart: 6, of which 5 were waited for; matrix products, arithmetic and copies ran while one was open for 13% of the time, Pallas kernels for 0%

commit v1 on v0

--- a/solution.py
+++ b/solution.py
@@ -92,7 +92,7 @@
     )
     hidden_back = partial_value
     grad_sum, hidden_back = (grad_sum, hidden_back)
-    hidden_back = lax.psum(hidden_back, "head")
+    hidden_back = jnp.sum(lax.all_gather(hidden_back, "head"), axis=0)
     masked = jnp.where(preact > 0, hidden_back, 0.0)
     in_grad = lax.dot_general(
         chosen.astype(jnp.float32),

time: 278 us -> 248 us (0.89)
  waiting for transfers between devices: 127 us -> 96.4 us
    psum x1 -> x0, waiting for transfers between devices: 55.7 us -> none  [local(): hidden_back = lax.psum(hidden_back, 'head')]
    all_gather x0 -> x1, waiting for transfers between devices: none -> 24.9 us  [local(): hidden_back = jnp.sum(lax.all_gather(hidden_back, 'head'), axis=0)]
  transfers between devices with their start and end apart: 6 -> 6, of which waited for: 5 -> 5; matrix products, arithmetic and copies ran while one was open for 13% -> 14% of each run, Pallas kernels for 0% -> 0%
where the time goes in v1:
time: 248 us; the launch traced here: 244 us
  waiting for transfers between devices  96.4 us (39%)
  matrix products  94.1 us (38%)
  between operations  16 us (6%)
  blocking collectives  14.9 us (6%)
  local copies, waits for them, and re-layouts  10.8 us (4%)
  other arithmetic  6.37 us (3%)
  starting transfers between devices  5.69 us (2%)
    reduce_scatter x1, waiting for transfers between devices, local(): lax.psum_scatter(jnp.dot(hidden_rows, head_weight, preferred_element_type...  32.6 us
    all_gather x1, waiting for transfers between devices, local(): hidden_back = jnp.sum(lax.all_gather(hidden_back, 'head'), axis=0)  24.9 us
    dot_general x6, matrix products, client_loss(): jnp.dot(low_rank, factor_b, precision=lax.Precision.HIGHEST)  21.5 us
    dot_general x1, matrix products, local(): lax.dot_general(received, head_weight, (((1,), (1,)), ((), ())), preferre...  16.1 us
    all_gather x1, waiting for transfers between devices, local(): lax.all_gather(byte_table, 'client', axis=1, tiled=True)  15.3 us
    all_gather x1, waiting for transfers between devices, local(): received = lax.all_gather(returned, 'client', axis=0, tiled=True)  14.9 us
    all_to_all x1, blocking collectives, local(): lax.all_to_all(deltas, 'head', split_axis=1, concat_axis=0, tiled=True)  14.9 us
    dot_general x1, matrix products, local(): lax.dot_general(hidden_rows, received, (((0,), (0,)), ((), ())), preferre...  14.9 us
  transfers between devices with their start and end apart: 6, of which 5 were waited for; matrix products, arithmetic and copies ran while one was open for 14% of the time, Pallas kernels for 0%

profile of v1, /device:TPU:0, one launch (start us, length us, event | category | flops | bytes accessed | tf_op | source)
XLA Modules:
  0.0 244.3 jit_solution(1335589572747601965)
XLA Ops:
  8.2 1.5 gather_fusion
  10.5 14.9 %fusion.59 = f32[32,16384]{1,0:T(8,128)} fusion(bf16[1024,16384]{1,0:T(8,128)(2,1)} %param.13, f32[32,1024]{1,0:T(8,128)S(1)} %convolution_add_fusion), kind=kOutput, calls=%fused_computation.91 | convolution fusion | flops 1073807360 | bytes 35782656 | tf_op jit(solution)/shard_map/dot_general | solution.py:71
  26.9 32.6 %reduce-scatter.2.cloned.1.call-done = f32[8,16384]{1,0:T(8,128)} async-done(((f32[32,16384]{1,0:T(8,128)}), f32[8,16384]{1,0:T(8,128)}) %reduce-scatter.2.cloned.1.call-update) | async-done | bytes 524304 | tf_op jit(solution)/shard_map/reduce_scatter | solution.py:70
  59.5 1.1 convert_bitcast_fusion
  61.9 0.9 reshape.182
  62.8 5.5 %all-to-all-start = ((bf16[8,2,8192]{2,1,0:T(2,128)(2,1)}), bf16[8,2,8192]{2,1,0:T(2,128)(2,1)S(1)}, u32[]{:S(2)}, u32[]{:S(2)}) async-start(bf16[8,2,8192]{2,1,0:T(2,128)(2,1)} %reshape.182), calls=%async_computation.1 | async-start | bytes 524288 | tf_op jit(solution)/shard_map/all_to_all | solution.py:76
  68.3 15.3 %all-gather.7.cloned.1.call-done = bf16[256,4096]{1,0:T(8,128)(2,1)} async-done(((bf16[256,1024]{1,0:T(8,128)(2,1)}), bf16[256,4096]{1,0:T(8,128)(2,1)}) %all-gather.7.cloned.1.call-update) | async-done | bytes 2097168 | tf_op jit(solution)/shard_map/all_gather | solution.py:62
  83.7 4.4 %multiply_reduce_fusion.2 = (f32[256]{0:T(256)S(1)}, f32[256,4096]{1,0:T(8,128)}) fusion(bf16[256,4096]{1,0:T(8,128)(2,1)} %all-gather.7.cloned.1.call-done, s32[256]{0:T(256)S(1)} %bitcast.45), kind=kOutput, calls=%fused_computation.34 | convolution fusion | flops 539033344 | bytes 6293504 | tf_op jit(solution)/shard_map/while/body/eval_jaxpr/dot_general | solution.py:41
  88.8 1.2 slice_reduce_fusion
  91.2 5.0 %fusion.18 = f32[256,16]{0,1:T(8,128)S(1)} fusion(bf16[4096,16]{1,0:T(8,128)(2,1)S(1)} %reshape.168, f32[256,4096]{1,0:T(8,128)} %get-tuple-element.34, f32[256]{0:T(256)S(1)} %add_rsqrt_fusion), kind=kOutput, calls=%fused_computation.39 | convolution fusion | flops 202375168 | bytes 4342784 | tf_op jit(solution)/shard_map/while/body/eval_jaxpr/jvp()/dot_general | solution.py:14
  96.3 4.3 %multiply_reduce_fusion.1 = (f32[256]{0:T(256)S(1)}, f32[256,4096]{1,0:T(8,128)}) fusion(f32[256,4096]{1,0:T(8,128)S(1)} %copy-done.2, f32[256,16]{0,1:T(8,128)S(1)} %fusion.18, bf16[16,4096]{1,0:T(8,128)(2,1)S(1)} %reshape.169), kind=kOutput, calls=%fused_computation.33 | convolution fusion | flops 205520640 | bytes 8537088 | tf_op jit(solution)/shard_map/while/body/eval_jaxpr/jvp()/dot_general | solution.py:15
  100.6 7.2 %all-gather.9.cloned.1.call-done = bf16[256,4096]{1,0:T(8,128)(2,1)} async-done(((bf16[256,1024]{1,0:T(8,128)(2,1)}), bf16[256,4096]{1,0:T(8,128)(2,1)}) %all-gather.9.cloned.1.call-update) | async-done | bytes 2097168 | tf_op jit(solution)/shard_map/all_gather | solution.py:63
  107.8 3.9 %fusion.78 = (f32[256]{0:T(256)S(1)}, f32[256,256]{0,1:T(8,128)S(1)}) fusion(bf16[256,4096]{1,0:T(8,128)(2,1)} %all-gather.9.cloned.1.call-done, f32[256,4096]{1,0:T(8,128)} %get-tuple-element.36, f32[256]{0:T(256)S(1)} %fusion.60), kind=kOutput, calls=%fused_computation.118 | convolution fusion | flops 539098880 | bytes 6555648 | tf_op jit(solution)/shard_map/while/body/eval_jaxpr/jvp()/dot_general | solution.py:21
  113.5 2.8 %fusion.76 = f32[256,16]{0,1:T(8,128)S(1)} fusion(bf16[16,4096]{1,0:T(8,128)(2,1)S(1)} %reshape.169, bf16[256,4096]{1,0:T(8,128)(2,1)S(1)} %get-tuple-element.40, f32[256,4096]{1,0:T(8,128)S(1)} %copy-done.4, f32[256]{0:T(256)S(1)} %multiply_multiply_fusion.1, f32[256]{0:T(256)S(1)} %fusion.60), kind=kOutput, calls=%fused_computation.117 | convolution fusion | flops 207618048 | bytes 6440960 | tf_op jit(solution)/shard_map/while/body/eval_jaxpr/transpose(jvp())/dot_general | solution.py:15
  116.3 3.1 %fusion.6 = f32[16,4096]{1,0:T(8,128)S(1)} fusion(f32[256,16]{0,1:T(8,128)S(1)} %fusion.18, bf16[16,4096]{1,0:T(8,128)(2,1)S(1)} %reshape.169, bf16[256,4096]{1,0:T(8,128)(2,1)S(1)} %get-tuple-element.40, f32[256,4096]{1,0:T(8,128)S(1)} %copy-done.4, f32[256]{0:T(256)S(1)} %multiply_multiply_fusion.1, f32[256]{0:T(256)S(1)} %fusion.60), kind=kOutput, calls=%fused_computation.21 | convolution fusion | flops 207814656 | bytes 6703104 | tf_op jit(solution)/shard_map/while/body/eval_jaxpr/transpose(jvp())/dot_general | solution.py:15
  119.4 2.5 %fusion.7 = f32[4096,16]{0,1:T(8,128)S(1)} fusion(f32[256,16]{0,1:T(8,128)S(1)} %fusion.76, f32[256,4096]{1,0:T(8,128)S(1)} %copy-done.3, f32[256]{0:T(256)S(1)} %add_rsqrt_fusion, bf16[4096,16]{0,1:T(8,128)(2,1)S(1)} %copy.24), kind=kOutput, calls=%fused_computation.23 | convolution fusion | flops 202571776 | bytes 4604928 | tf_op jit(solution)/shard_map/while/body/eval_jaxpr/transpose(jvp())/dot_general | solution.py:14
  121.9 3.4 %fusion.15 = f32[256,16]{0,1:T(8,128)S(1)} fusion(f32[4096,16]{0,1:T(8,128)S(1)} %fusion.7, f32[256,4096]{1,0:T(8,128)S(1)} %copy-done.3, f32[256]{0:T(256)S(1)} %add_rsqrt_fusion), kind=kOutput, calls=%fused_computation.36 | convolution fusion | flops 202375168 | bytes 4473856 | tf_op jit(solution)/shard_map/while/body/eval_jaxpr/jvp()/dot_general | solution.py:14
  125.4 4.1 %multiply_reduce_fusion = (f32[256]{0:T(256)S(1)}, f32[256,4096]{1,0:T(8,128)S(1)}) fusion(f32[256,4096]{1,0:T(8,128)S(1)} %copy-done.3, f32[256,16]{0,1:T(8,128)S(1)} %fusion.15, f32[16,4096]{1,0:T(8,128)S(1)} %fusion.6), kind=kOutput, calls=%fused_computation.31 | convolution fusion | flops 205520640 | bytes 8668160 | tf_op jit(solution)/shard_map/while/body/eval_jaxpr/jvp()/dot_general | solution.py:15
  130.4 0.9 fusion.11
  131.4 4.2 %fusion.73 = f32[256,16]{0,1:T(8,128)S(1)} fusion(f32[16,4096]{1,0:T(8,128)S(1)} %fusion.6, bf16[256,4096]{1,0:T(8,128)(2,1)S(1)} %get-tuple-element.46, f32[256,4096]{1,0:T(8,128)S(1)} %get-tuple-element.42, f32[256]{0:T(256)S(1)} %multiply_multiply_fusion, f32[256]{0:T(256)S(1)} %fusion.61), kind=kOutput, calls=%fused_computation.116 | convolution fusion | flops 207618048 | bytes 6572032 | tf_op jit(solution)/shard_map/while/body/eval_jaxpr/transpose(jvp())/dot_general | solution.py:15
  135.6 2.9 %fusion.9 = bf16[16,4096]{1,0:T(8,128)(2,1)S(1)} fusion(f32[16,4096]{1,0:T(8,128)S(1)} %fusion.6, f32[256,16]{0,1:T(8,128)S(1)} %fusion.15, bf16[16,4096]{1,0:T(8,128)(2,1)S(1)} %reshape.169, bf16[256,4096]{1,0:T(8,128)(2,1)S(1)} %get-tuple-element.46, f32[256,4096]{1,0:T(8,128)S(1)} %get-tuple-element.42, f32[256]{0:T(256)S(1)} %multiply_multiply_fusion, ...), kind=kOutput, calls=%fused_computation.25 | convolution fusion | flops 207945728 | bytes 6834176 | tf_op jit(solution)/shard_map/while/body/eval_jaxpr/transpose(jvp())/dot_general | solution.py:15
  138.5 2.5 %fusion.8 = bf16[4096,16]{0,1:T(8,128)(2,1)S(1)} fusion(f32[4096,16]{0,1:T(8,128)S(1)} %fusion.7, f32[256,16]{0,1:T(8,128)S(1)} %fusion.73, f32[256,4096]{1,0:T(8,128)S(1)} %copy-done.3, f32[256]{0:T(256)S(1)} %add_rsqrt_fusion, bf16[4096,16]{0,1:T(8,128)(2,1)S(1)} %copy.24), kind=kOutput, calls=%fused_computation.24 | convolution fusion | flops 202702848 | bytes 4736000 | tf_op jit(solution)/shard_map/while/body/eval_jaxpr/transpose(jvp())/dot_general | solution.py:14
  141.5 1.2 concatenate.17
  143.4 2.2 reduce.5
  145.8 14.9 %all_to_all.26 = bf16[8,2,8192]{2,1,0:T(2,128)(2,1)S(1)} all-to-all(bf16[8,2,8192]{2,1,0:T(2,128)(2,1)S(1)} %reshape.184), channel_id=1, replica_groups=mesh['head'=8,'client'=4] {'head'}, dimensions={0} | all-to-all | bytes 524288 | tf_op jit(solution)/shard_map/all_to_all | solution.py:84
  161.0 1.0 copy.27
  162.1 14.9 %all-gather.11.cloned.1.call-done = bf16[1,32,16384]{2,1,0:T(8,128)(2,1)} async-done(((bf16[1,8,16384]{2,1,0:T(8,128)(2,1)}), bf16[1,32,16384]{2,1,0:T(8,128)(2,1)}) %all-gather.11.cloned.1.call-update) | async-done | bytes 1048592 | tf_op jit(solution)/shard_map/all_gather | solution.py:85
  177.0 16.1 %fusion.30 = f32[32,1024]{1,0:T(8,128)} fusion(bf16[1024,16384]{1,0:T(8,128)(2,1)} %param.13, bf16[1,32,16384]{2,1,0:T(8,128)(2,1)} %all-gather.11.cloned.1.call-done), kind=kOutput, calls=%fused_computation.52 | convolution fusion | flops 1073741824 | bytes 34734080 | tf_op jit(solution)/shard_map/dot_general | solution.py:90
  193.6 14.9 %convolution_convert_fusion = bf16[1024,16384]{1,0:T(8,128)(2,1)} fusion(bf16[1,32,16384]{2,1,0:T(8,128)(2,1)S(1)} %copy-done.6, f32[32,1024]{1,0:T(8,128)S(1)} %convolution_add_fusion), kind=kOutput, calls=%fused_computation.1 | convolution fusion | flops 1090584576 | bytes 34734080 | tf_op jit(solution)/shard_map/dot_general | solution.py:87
  208.5 24.9 %all-gather.13.cloned.1.call-done = f32[256,1024]{1,0:T(8,128)} async-done(((f32[32,1024]{1,0:T(8,128)}), f32[256,1024]{1,0:T(8,128)}) %all-gather.13.cloned.1.call-update) | async-done | bytes 1048592 | tf_op jit(solution)/shard_map/all_gather | solution.py:95
  233.5 1.3 reduce_sum.120
  234.8 1.6 fusion.42
  (60 shorter events, 11.2 us)
Async XLA Ops:
  7.2 2.5 %copy-start = (bf16[256,1024]{1,0:T(8,128)(2,1)S(1)}, bf16[256,1024]{1,0:T(8,128)(2,1)}, u32[]{:S(2)}) copy-start(bf16[256,1024]{1,0:T(8,128)(2,1)} %param.11) | copy-start | bytes 1572868
  7.2 52.3 %reduce-scatter.2.cloned.1.call-start = ((), (), s32[]{:S(2)}) async-start(), calls=%async_computation.3 | async-start | bytes 2621440 | tf_op jit(solution)/shard_map/reduce_scatter | solution.py:70
  25.4 58.2 %copy-start.7 = (s32[1,256]{1,0:T(1,128)S(1)}, s32[1,256]{1,0:T(1,128)}, u32[]{:S(2)}) copy-start(s32[1,256]{1,0:T(1,128)} %param.14) | copy-start | bytes 3076
  25.4 58.2 %all-gather.7.cloned.1.call-start = ((), (), s32[]{:S(2)}) async-start(), calls=%async_computation.4 | async-start | bytes 2621440 | tf_op jit(solution)/shard_map/all_gather | solution.py:62
  26.2 81.6 %all-gather.9.cloned.1.call-start = ((), (), s32[]{:S(2)}) async-start(), calls=%async_computation.5 | async-start | bytes 2621440 | tf_op jit(solution)/shard_map/all_gather | solution.py:63
  62.8 25.2 %all-to-all-start = ((bf16[8,2,8192]{2,1,0:T(2,128)(2,1)}), bf16[8,2,8192]{2,1,0:T(2,128)(2,1)S(1)}, u32[]{:S(2)}, u32[]{:S(2)}) async-start(bf16[8,2,8192]{2,1,0:T(2,128)(2,1)} %reshape.182), calls=%async_computation.1 | async-start | bytes 524288 | tf_op jit(solution)/shard_map/all_to_all | solution.py:76
  68.3 108.7 %all-gather.11.cloned.1.call-start = ((), (), s32[]{:S(2)}) async-start(), calls=%async_computation.6 | async-start | bytes 1310720 | tf_op jit(solution)/shard_map/all_gather | solution.py:85
  91.2 5.1 %copy-start.2 = (f32[256,4096]{1,0:T(8,128)S(1)}, f32[256,4096]{1,0:T(8,128)}, u32[]{:S(2)}) copy-start(f32[256,4096]{1,0:T(8,128)} %get-tuple-element.34) | copy-start | bytes 12582916
  100.6 11.1 %copy-start.8 = (s32[1,256]{1,0:T(1,128)S(1)}, s32[1,256]{1,0:T(1,128)}, u32[]{:S(2)}) copy-start(s32[1,256]{1,0:T(1,128)} %param.15) | copy-start | bytes 3076
  107.8 4.6 %copy-start.4 = (f32[256,4096]{1,0:T(8,128)S(1)}, f32[256,4096]{1,0:T(8,128)}, u32[]{:S(2)}) copy-start(f32[256,4096]{1,0:T(8,128)} %get-tuple-element.36) | copy-start | bytes 12582916
  107.8 4.7 %copy-start.5 = (bf16[256,4096]{1,0:T(8,128)(2,1)S(1)}, bf16[256,4096]{1,0:T(8,128)(2,1)}, u32[]{:S(2)}) copy-start(bf16[256,4096]{1,0:T(8,128)(2,1)} %all-gather.9.cloned.1.call-done) | copy-start | bytes 6291460
  116.3 3.1 %copy-start.3 = (f32[256,4096]{1,0:T(8,128)S(1)}, f32[256,4096]{1,0:T(8,128)}, u32[]{:S(2)}) copy-start(f32[256,4096]{1,0:T(8,128)} %get-tuple-element.34) | copy-start | bytes 12582916
  162.0 71.4 %all-gather.13.cloned.1.call-start = ((), (), s32[]{:S(2)}) async-start(), calls=%async_computation.7 | async-start | bytes 1179648 | tf_op jit(solution)/shard_map/all_gather | solution.py:95
  177.0 16.7 %copy-start.6 = (bf16[1,32,16384]{2,1,0:T(8,128)(2,1)S(1)}, bf16[1,32,16384]{2,1,0:T(8,128)(2,1)}, u32[]{:S(2)}) copy-start(bf16[1,32,16384]{2,1,0:T(8,128)(2,1)} %all-gather.11.cloned.1.call-done) | copy-start | bytes 3145732
  193.6 42.7 %copy-start.1 = (bf16[256,1024]{1,0:T(8,128)(2,1)S(1)}, bf16[256,1024]{1,0:T(8,128)(2,1)}, u32[]{:S(2)}) copy-start(bf16[256,1024]{1,0:T(8,128)(2,1)} %param.11) | copy-start | bytes 1572868
Sparse Core Ops, SparseCore 0:
  25.6 33.9 reduce-scatter.1
  61.1 22.5 all-gather.6
  85.2 22.5 all-gather.8
  162.1 14.7 all-gather.10
  193.2 40.2 all-gather.12
